TPU v7x, 32 devices: a whole 2x2x4 slice. The times are simulated.
32 devices in a mesh: parts: 2 (over x), dp: 16 (over z, y, core).
Axes of the slice: x: 2, y: 2, z: 4, core: 2. Of those that a mesh axis runs over, the one named last changes fastest.
Arguments:
- activations: bfloat16 [8192, 14336], P(('parts', 'dp')), parts along dimension 0, may hold values from -6 to 6
- out_grads: bfloat16 [8192, 4096], P(('parts', 'dp')), parts along dimension 0, may hold values from -6 to 6
- lengths: int32 [32, 4], P(('parts', 'dp')), parts along dimension 0, may hold values from 1 to 128, 256 in all within a row
- proj_in: bfloat16 [14336, 64], replicated, may hold values from -0.046875 to 0.046875
- proj_out: bfloat16 [4096, 64], replicated, may hold values from -0.09375 to 0.09375
- queries: bfloat16 [1024, 4096], P(('parts', 'dp')), parts along dimension 0, may hold values from -0.01171875 to 0.01171875
Outputs:
- scores: bfloat16 [128, 512], P(('parts', 'dp')), parts along dimension 0
There are 2 independent parts, one for each index of `parts`. A program takes and returns all parts, laid end to end along the dimension named above; an argument that names none is the same for every part. Nothing has to cross between parts.
Inputs may be any that keep to these rules, and one draw needn't show every extreme that they name: Each row of lengths sums to 256, and one entry of each row equals 128.
All inputs are finite; a program needn't handle non-finite values.
Results may differ from a plain program's by a relative error of at most 0.0065.
Values may be sent and summed in bfloat16 or wider, within the bound.
A program may use at most 128 MiB of HBM per device.

v0:
```python
import jax
import jax.numpy as jnp
from jax import lax
from jax.sharding import PartitionSpec as P


def local(activations, out_grads, lengths, proj_in, proj_out, queries):
    tok_count = activations.shape[0]
    rank_size = proj_in.shape[1]
    proj_acts = jnp.dot(activations, proj_in, preferred_element_type=jnp.float32).astype(
        jnp.bfloat16
    )
    proj_grads = jnp.dot(out_grads, proj_out, preferred_element_type=jnp.float32).astype(
        jnp.bfloat16
    )
    counts = lengths[0]
    tok_ends = jnp.cumsum(counts)
    tok_starts = tok_ends - counts
    position = jnp.arange(tok_count, dtype=jnp.int32)
    member = (
        (position[None, :] >= tok_starts[:, None]) & (position[None, :] < tok_ends[:, None])
    ).astype(jnp.bfloat16)
    masked_grads = member[:, :, None] * proj_grads[None, :, :]
    summed = jnp.einsum("eti,tj->eij", masked_grads, proj_acts, preferred_element_type=jnp.float32)
    example_grads = summed.reshape(counts.shape[0], rank_size * rank_size).astype(jnp.bfloat16)
    contract = (((1,), (1,)), ((), ()))
    local_scores = lax.dot_general(
        lax.all_gather(example_grads, "dp", axis=0, tiled=True),
        queries,
        contract,
        preferred_element_type=jnp.float32,
    ).astype(jnp.bfloat16)
    return lax.all_to_all(local_scores, "dp", split_axis=0, concat_axis=1, tiled=True)


def solution(mesh):
    in_specs = (
        P(("parts", "dp"), None),
        P(("parts", "dp"), None),
        P(("parts", "dp"), None),
        P(),
        P(),
        P(("parts", "dp"), None),
    )
    out_specs = P(("parts", "dp"), None)
    return jax.shard_map(local, mesh=mesh, in_specs=in_specs, out_specs=out_specs, check_vma=False)
```

profile of v0, /device:TPU:0, one launch (start us, length us, event | category | flops | bytes accessed | tf_op | source)
XLA Modules:
  0.0 44.8 jit_solution(8421804942782179360)
XLA Ops:
  0.0 0.0 copy-start
  0.0 1.0 %reduce-window.7 = s32[4,1]{0,1:T(1,128)S(1)} reduce-window(s32[4,1]{0,1:T(1,128)} %bitcast.20, s32[]{:T(128)} %constant.3.clone.1), window={size=4x1 pad=3_0x0_0}, to_apply=%region_0.0 | reduce-window | flops 12 | bytes 36 | tf_op jit(solution)/shard_map/reduce-window.2
  1.0 0.7 %bitcast_subtract_fusion = s32[4]{0:T(128)S(1)} fusion(s32[1,4]{1,0:T(1,128)} %param.8, s32[4,1]{0,1:T(1,128)S(1)} %reduce-window.7), kind=kLoop, calls=%fused_computation.12 | loop fusion | flops 4 | bytes 48 | tf_op jit(solution)/shard_map/sub | solution.py:18
  1.6 0.1 fusion.5
  1.7 0.0 copy-done
  1.7 1.8 %convolution_convert_fusion.2 = bf16[256,64]{0,1:T(8,128)(2,1)S(1)} fusion(bf16[256,4096]{1,0:T(8,128)(2,1)S(1)} %copy-done, bf16[4096,64]{0,1:T(8,128)(2,1)} %param.10), kind=kOutput, calls=%fused_computation.2 | convolution fusion | flops 134234112 | bytes 2654208 | tf_op jit(solution)/shard_map/dot_general | solution.py:13
  3.5 0.0 copy-start.1
  3.5 6.2 %convolution_convert_fusion = bf16[4,64,64]{2,1,0:T(8,128)(2,1)S(1)} fusion(bf16[256,14336]{1,0:T(8,128)(2,1)} %param.6, bf16[14336,64]{0,1:T(8,128)(2,1)} %param.9, bf16[256,64]{0,1:T(8,128)(2,1)S(1)} %convolution_convert_fusion.2, bf16[4,256]{1,0:T(4,128)(2,1)S(1)} %fusion.5), kind=kOutput, calls=%fused_computation | convolution fusion | flops 478248960 | bytes 9242624 | tf_op jit(solution)/shard_map/eti,tj->eij/dot_general | solution.py:24
  9.7 0.1 reshape.80
  9.9 24.6 %all-gather = bf16[16,4,4096]{2,1,0:T(4,128)(2,1)S(1)} all-gather(bf16[1,4,4096]{2,1,0:T(4,128)(2,1)S(1)} %reshape.80), channel_id=1, replica_groups=mesh['parts'=2,'dp'=16] {'dp'}, dimensions={0}, use_global_device_ids=true | all-gather | bytes 557056 | tf_op jit(solution)/shard_map/all_gather | solution.py:28
  34.5 0.1 reshape.81
  34.6 0.0 copy-done.1
  34.6 0.3 convolution_convert_fusion.3
  34.9 0.1 copy.11
  35.0 9.1 %all_to_all.19 = bf16[16,4,32]{2,1,0:T(4,128)(2,1)S(1)} all-to-all(bf16[16,4,32]{2,1,0:T(4,128)(2,1)S(1)} %bitcast.17), channel_id=1, replica_groups=mesh['parts'=2,'dp'=16] {'dp'}, dimensions={0} | all-to-all | bytes 8192 | tf_op jit(solution)/shard_map/all_to_all | solution.py:33
  44.1 0.7 %all_to_all.17 = bf16[4,512]{1,0:T(4,128)(2,1)} reshape(bf16[4,16,32]{2,1,0:T(8,128)(2,1)S(1)} %copy.12) | data formatting | bytes 8192 | tf_op jit(solution)/shard_map/all_to_all | solution.py:33
  (1 shorter events, 0.0 us)
Async XLA Ops:
  0.0 1.7 %copy-start = (bf16[256,4096]{1,0:T(8,128)(2,1)S(1)}, bf16[256,4096]{1,0:T(8,128)(2,1)}, u32[]{:S(2)}) copy-start(bf16[256,4096]{1,0:T(8,128)(2,1)} %param.7) | copy-start | bytes 6291460
  3.5 31.1 %copy-start.1 = (bf16[32,4096]{1,0:T(8,128)(2,1)S(1)}, bf16[32,4096]{1,0:T(8,128)(2,1)}, u32[]{:S(2)}) copy-start(bf16[32,4096]{1,0:T(8,128)(2,1)} %param.11) | copy-start | bytes 786436
where the time goes:
time: 45 us; the launch traced here: 44.8 us
  blocking collectives  33.7 us (75%)
  matrix products  8.27 us (18%)
  other arithmetic  1.71 us (4%)
  local copies, waits for them, and re-layouts  1.04 us (2%)
    all_gather x1, blocking collectives, local(): lax.all_gather(example_grads, 'dp', axis=0, tiled=True)  24.6 us
    all_to_all x1, blocking collectives, local(): lax.all_to_all(local_scores, 'dp', split_axis=0, concat_axis=1, tiled=True)  9.07 us
    dot_general x1, matrix products, local(): jnp.einsum('eti,tj->eij', masked_grads, proj_acts, preferred_element_type...  6.21 us
    dot_general x1, matrix products, local(): jnp.dot(out_grads, proj_out, preferred_element_type=jnp.float32)  1.8 us
    another operation x1, other arithmetic  0.97 us

commit v1 on v0

v1 whole, which is shorter than its diff:
```python
import functools

import jax
import jax.numpy as jnp
from jax import lax
from jax.experimental import pallas as pl
from jax.experimental.pallas import tpu as pltpu
from jax.sharding import PartitionSpec as P

MESH = pl.DeviceIdType.MESH
NT = (((1,), (1,)), ((), ()))
NN = (((1,), (0,)), ((), ()))
CHUNKS = 4
PIECES = 2
GROUP = 4


def kernel(
    n,
    lens,
    acts_hbm,
    grads_hbm,
    win_hbm,
    wout_hbm,
    q_hbm,
    out_ref,
    acts,
    grads,
    win,
    wout,
    qs,
    rows,
    masks,
    expand,
    acc,
    stage,
    result,
    local_sem,
    acts_sem,
    grads_sem,
    q_send,
    q_recv,
    row_send,
    row_recv,
    mask_send,
    mask_recv,
    res_send,
    res_recv,
):
    me = lax.axis_index("dp")
    n_groups = n // GROUP
    group, lane = me // GROUP, lax.rem(me, GROUP)
    n_half, _, per_half, chunk, width = rows.shape
    ex = stage.shape[1]
    rank = width // 2
    pairs = rank // 2
    half, slot = group // per_half, lax.rem(group, per_half)
    ff = acts.shape[1]
    piece = ff // PIECES

    def peer(t):
        return lax.rem(group + t, n_groups) * GROUP + lane

    buddy = me + 1 - 2 * lax.rem(me, 2)
    across = me + 2 - 4 * lax.rem(me // 2, 2)
    across_lane = lax.rem(across, GROUP)

    load_q = pltpu.make_async_copy(q_hbm, qs.at[lane], local_sem.at[0])
    load_q.start()
    load_wout = pltpu.make_async_copy(wout_hbm, wout, local_sem.at[1])
    load_win = pltpu.make_async_copy(win_hbm, win, local_sem.at[2])
    load_wout.start()
    load_win.start()
    load_grads, load_acts = [], []
    for c in range(CHUNKS):
        span = pl.ds(c * chunk, chunk)
        load = pltpu.make_async_copy(grads_hbm.at[span], grads.at[span], grads_sem.at[c])
        load.start()
        load_grads.append(load)
        for p in range(PIECES):
            cols = pl.ds(p * piece, piece)
            load = pltpu.make_async_copy(
                acts_hbm.at[span, cols], acts.at[span, cols], acts_sem.at[c, p]
            )
            load.start()
            load_acts.append(load)

    barrier = pltpu.get_barrier_semaphore()
    peers = [peer(t) for t in range(1, n_groups)]
    for other in peers + [buddy, across]:
        pl.semaphore_signal(barrier, inc=1, device_id={"dp": other}, device_id_type=MESH)

    row_id = lax.broadcasted_iota(jnp.int32, (8, width), 0) - slot * ex
    lane_id = lax.broadcasted_iota(jnp.int32, (8, width), 1) - slot * chunk
    inside = (lane_id >= 0) & (lane_id < chunk)
    for c in range(CHUNKS):
        token = lane_id + c * chunk
        start = jnp.int32(0)
        mask = jnp.zeros((8, width), jnp.float32)
        for e in range(ex):
            end = start + lens[0, e]
            hit = inside & (row_id == e) & (token >= start) & (token < end)
            mask = jnp.where(hit, 1.0, mask)
            start = end
        masks[group, c] = mask
    r_id = lax.broadcasted_iota(jnp.int32, (16 * pairs, width), 0)
    c_id = lax.broadcasted_iota(jnp.int32, (16 * pairs, width), 1)
    odd = (r_id >= 8 * pairs).astype(jnp.int32)
    source = 2 * ((r_id - odd * 8 * pairs) // 8) + odd
    expand[...] = jnp.where(source == c_id, 1.0, 0.0).astype(jnp.bfloat16)
    acc[...] = jnp.zeros_like(acc)

    pl.semaphore_wait(barrier, len(peers) + 2)

    load_q.wait()
    q_copies = []
    for i, other in enumerate((across, buddy)):
        copy = pltpu.make_async_remote_copy(
            src_ref=qs.at[lane],
            dst_ref=qs.at[lane],
            send_sem=q_send.at[i],
            recv_sem=q_recv.at[i],
            device_id={"dp": other},
            device_id_type=MESH,
        )
        copy.start()
        q_copies.append(copy)
    mask_copies = []
    for t in range(1, n_groups):
        copy = pltpu.make_async_remote_copy(
            src_ref=masks.at[group],
            dst_ref=masks.at[group],
            send_sem=mask_send.at[t - 1],
            recv_sem=mask_recv.at[t - 1],
            device_id={"dp": peer(t)},
            device_id_type=MESH,
        )
        copy.start()
        mask_copies.append(copy)

    load_wout.wait()
    load_win.wait()
    row_copies = []
    for c in range(CHUNKS):
        span = pl.ds(c * chunk, chunk)
        load_grads[c].wait()
        g = lax.dot_general(grads[span], wout[...], NT, preferred_element_type=jnp.float32)
        a = jnp.zeros((chunk, rank), jnp.float32)
        for p in range(PIECES):
            load_acts[c * PIECES + p].wait()
            cols = pl.ds(p * piece, piece)
            a = a + lax.dot_general(
                acts[span, cols], win[:, cols], NT, preferred_element_type=jnp.float32
            )
        rows[half, c, slot] = jnp.concatenate([g, a], axis=1).astype(jnp.bfloat16)
        copies = []
        for t in range(1, n_groups):
            copy = pltpu.make_async_remote_copy(
                src_ref=rows.at[half, c, slot],
                dst_ref=rows.at[half, c, slot],
                send_sem=row_send.at[t - 1, c],
                recv_sem=row_recv.at[t - 1, c],
                device_id={"dp": peer(t)},
                device_id_type=MESH,
            )
            copy.start()
            copies.append(copy)
        row_copies.append(copies)

    def gather(c):
        for copy in row_copies[c]:
            copy.wait_recv()
        for h in range(n_half):
            block = rows[h, c].reshape(per_half * chunk, width)
            mask = masks[h * per_half, c]
            for s in range(1, per_half):
                mask = mask + masks[h * per_half + s, c]
            wide = lax.dot_general(expand[...], block, NT, preferred_element_type=jnp.float32)
            wide = wide.reshape(2 * pairs, 8, width) * mask[None]
            wide = wide.reshape(16 * pairs, width).astype(jnp.bfloat16)
            acc[h] += lax.dot_general(wide, block, NN, preferred_element_type=jnp.float32)

    for copy in mask_copies:
        copy.wait_recv()
    gather(0)
    gather(1)
    q_copies[0].wait_recv()
    relay = pltpu.make_async_remote_copy(
        src_ref=qs.at[across_lane],
        dst_ref=qs.at[across_lane],
        send_sem=q_send.at[2],
        recv_sem=q_recv.at[2],
        device_id={"dp": buddy},
        device_id_type=MESH,
    )
    relay.start()
    for c in range(2, CHUNKS):
        gather(c)

    lower = lax.broadcasted_iota(jnp.int32, (8, width), 1) < rank
    columns = []
    for k in range(pairs):
        parts = []
        for h in range(n_half):
            even = pltpu.roll(acc[h, 8 * k : 8 * k + 8], rank, 1)
            odd_rows = acc[h, 8 * pairs + 8 * k : 8 * pairs + 8 * k + 8]
            parts.append(jnp.where(lower, even, odd_rows))
        columns.append(jnp.concatenate(parts, axis=0).astype(jnp.bfloat16))
    example_grads = jnp.concatenate(columns, axis=1)
    q_copies[1].wait_recv()
    relay.wait_recv()
    queries = qs[...].reshape(qs.shape[0] * qs.shape[1], qs.shape[2])
    scores = lax.dot_general(example_grads, queries, NT, preferred_element_type=jnp.float32)
    for s in range(n_groups):
        stage[s] = scores[s * ex : (s + 1) * ex].astype(jnp.bfloat16)
    res_copies = []
    for t in range(1, n_groups):
        copy = pltpu.make_async_remote_copy(
            src_ref=stage.at[lax.rem(group + t, n_groups)],
            dst_ref=result.at[group],
            send_sem=res_send.at[t - 1],
            recv_sem=res_recv.at[t - 1],
            device_id={"dp": peer(t)},
            device_id_type=MESH,
        )
        copy.start()
        res_copies.append(copy)
    result[group] = stage[group]
    for copy in res_copies:
        copy.wait_recv()
    cols = qs.shape[0] * qs.shape[1]
    for s in range(n_groups):
        out_ref[:, s * cols : (s + 1) * cols] = result[s]
    for copy in q_copies + [relay] + mask_copies + res_copies:
        copy.wait_send()
    for copies in row_copies:
        for copy in copies:
            copy.wait_send()


def local(n, activations, out_grads, lengths, proj_in, proj_out, queries):
    tokens, ff = activations.shape
    d = out_grads.shape[1]
    rank = proj_in.shape[1]
    ex = lengths.shape[1]
    nq, params = queries.shape
    n_groups = n // GROUP
    per_half = 8 // ex
    n_half = n_groups // per_half
    chunk = tokens // CHUNKS
    width = 2 * rank
    bf16, f32 = jnp.bfloat16, jnp.float32
    dma = pltpu.SemaphoreType.DMA
    others = n_groups - 1
    hbm = pl.BlockSpec(memory_space=pltpu.MemorySpace.HBM)
    return pl.pallas_call(
        functools.partial(kernel, n),
        out_shape=jax.ShapeDtypeStruct((ex, nq * n), bf16),
        in_specs=[pl.BlockSpec(memory_space=pltpu.MemorySpace.SMEM)] + [hbm] * 5,
        out_specs=pl.BlockSpec(memory_space=pltpu.MemorySpace.VMEM),
        scratch_shapes=[
            pltpu.VMEM((tokens, ff), bf16),
            pltpu.VMEM((tokens, d), bf16),
            pltpu.VMEM((rank, ff), bf16),
            pltpu.VMEM((rank, d), bf16),
            pltpu.VMEM((GROUP, nq, params), bf16),
            pltpu.VMEM((n_half, CHUNKS, per_half, chunk, width), bf16),
            pltpu.VMEM((n_groups, CHUNKS, 8, width), f32),
            pltpu.VMEM((8 * rank, width), bf16),
            pltpu.VMEM((n_half, 8 * rank, width), f32),
            pltpu.VMEM((n_groups, ex, GROUP * nq), bf16),
            pltpu.VMEM((n_groups, ex, GROUP * nq), bf16),
            dma((3,)),
            dma((CHUNKS, PIECES)),
            dma((CHUNKS,)),
            dma((3,)),
            dma((3,)),
            dma((others, CHUNKS)),
            dma((others, CHUNKS)),
            dma((others,)),
            dma((others,)),
            dma((others,)),
            dma((others,)),
        ],
        compiler_params=pltpu.CompilerParams(
            collective_id=0, has_side_effects=True, vmem_limit_bytes=60 * 1024 * 1024
        ),
    )(lengths, activations, out_grads, proj_in.T, proj_out.T, queries)


def solution(mesh):
    in_specs = (
        P(("parts", "dp"), None),
        P(("parts", "dp"), None),
        P(("parts", "dp"), None),
        P(),
        P(),
        P(("parts", "dp"), None),
    )
    out_specs = P(("parts", "dp"), None)
    body = functools.partial(local, mesh.shape["dp"])
    return jax.shard_map(body, mesh=mesh, in_specs=in_specs, out_specs=out_specs, check_vma=False)
```

time: 45 us -> 24.5 us (0.54)
  blocking collectives: 33.7 us -> 0 us
  Pallas kernels: 0 us -> 23 us
  matrix products: 8.27 us -> 0 us
  other arithmetic: 1.71 us -> 0 us
    all_gather x1 -> x0, blocking collectives: 24.6 us -> none  [local(): lax.all_gather(example_grads, 'dp', axis=0, tiled=True)]
    pallas_call x0 -> x1, Pallas kernels: none -> 23 us  [local(): pl.pallas_call(functools.partial(kernel, n), out_shape=jax.ShapeDtypeStru...]
    all_to_all x1 -> x0, blocking collectives: 9.07 us -> none  [local(): lax.all_to_all(local_scores, 'dp', split_axis=0, concat_axis=1, tiled=True)]
    dot_general x3 -> x0, matrix products: 8.27 us -> none  [the longest x1 6.21 us: local(): jnp.einsum('eti,tj->eij', masked_grads, proj_acts, preferred_element_type...]
    unnamed x6 -> x1, local copies, waits for them, and re-layouts: 0.24 us -> 1.28 us
    another operation x1 -> x0, other arithmetic: 0.97 us -> none
    all_to_all x2 -> x0, local copies, waits for them, and re-layouts: 0.69 us -> none  [local(): lax.all_to_all(local_scores, 'dp', split_axis=0, concat_axis=1, tiled=True)]
    sub x1 -> x0, other arithmetic: 0.66 us -> none  [local(): tok_starts = tok_ends - counts]
where the time goes in v1:
time: 24.5 us; the launch traced here: 24.3 us
  Pallas kernels  23 us (94%)
  local copies, waits for them, and re-layouts  1.28 us (5%)
    pallas_call x1, Pallas kernels, local(): pl.pallas_call(functools.partial(kernel, n), out_shape=jax.ShapeDtypeStru...  23 us
    unnamed x1, local copies, waits for them, and re-layouts  1.28 us

profile of v1, /device:TPU:0, one launch (start us, length us, event | category | flops | bytes accessed | tf_op | source)
XLA Modules:
  0.0 24.3 jit_solution(11512001363980126712)
XLA Ops:
  0.0 23.0 %shard_map.64 = bf16[4,512]{1,0:T(4,128)(2,1)} custom-call(s32[1,4]{1,0:T(1,128)} %lens.1, bf16[256,14336]{1,0:T(8,128)(2,1)} %acts_hbm.1, bf16[256,4096]{1,0:T(8,128)(2,1)} %grads_hbm.1, bf16[64,14336]{1,0:T(8,128)(2,1)} %bitcast.2, bf16[64,4096]{1,0:T(8,128)(2,1)} %bitcast.3, bf16[32,4096]{1,0:T(8,128)(2,1)} %q_hbm.1), custom_call_target="tpu_custom_call" | custom-call | tf_op jit(solution)/shard_map/pallas_call | solution.py:256
  23.1 1.3 %copy.8 = bf16[4,512]{1,0:T(4,128)(2,1)} copy(bf16[4,512]{1,0:T(4,128)(2,1)} %shard_map.64) | data formatting | bytes 8192

commit v2 on v1

v2 whole, which is shorter than its diff:
```python
import functools

import jax
import jax.numpy as jnp
from jax import lax
from jax.experimental import pallas as pl
from jax.experimental.pallas import tpu as pltpu
from jax.sharding import PartitionSpec as P

MESH = pl.DeviceIdType.MESH
NT = (((1,), (1,)), ((), ()))
NN = (((1,), (0,)), ((), ()))
CHUNKS = (4, 8, 4)
PIECES = 4
GROUP = 4


def kernel(
    n,
    lens_hbm,
    acts_hbm,
    grads_hbm,
    win_hbm,
    wout_hbm,
    q_hbm,
    out_hbm,
    lens,
    acts,
    grads,
    win,
    wout,
    qs,
    expand,
    acc,
    stage,
    result,
    out_vmem,
    local_sem,
    acts_sem,
    grads_sem,
    win_sem,
    q_send,
    q_recv,
    row_send,
    row_recv,
    mask_send,
    mask_recv,
    res_send,
    res_recv,
    *per_chunk,
):
    count = len(per_chunk) // 2
    rows, masks = per_chunk[:count], per_chunk[count:]
    me = lax.axis_index("dp")
    n_groups = n // GROUP
    group, lane = me // GROUP, lax.rem(me, GROUP)
    n_half, per_half, _, width = rows[0].shape
    sizes = [ref.shape[2] for ref in rows]
    starts = [sum(sizes[:c]) for c in range(count)]
    ex = stage.shape[1]
    rank = width // 2
    pairs = rank // 2
    half, slot = group // per_half, lax.rem(group, per_half)
    ff = acts.shape[1]
    piece = ff // PIECES

    def peer(t):
        return lax.rem(group + t, n_groups) * GROUP + lane

    buddy = me + 1 - 2 * lax.rem(me, 2)
    across = me + 2 - 4 * lax.rem(me // 2, 2)
    across_lane = lax.rem(across, GROUP)

    def start(source, target, sem):
        load = pltpu.make_async_copy(source, target, sem)
        load.start()
        return load

    pieces = [pl.ds(p * piece, piece) for p in range(PIECES)]
    spans = [pl.ds(starts[c], sizes[c]) for c in range(count)]
    load_grads, load_acts = {}, {}

    def fetch_grads(c):
        span = spans[c]
        load_grads[c] = start(grads_hbm.at[span], grads.at[span], grads_sem.at[c])

    def fetch_acts(c, p):
        part = (spans[c], pieces[p])
        load_acts[c, p] = start(acts_hbm.at[*part], acts.at[*part], acts_sem.at[c, p])

    def fetch(c):
        if c < count:
            fetch_grads(c)
            for p in range(PIECES):
                fetch_acts(c, p)

    load_win = []
    for p in range(PIECES):
        part = win.at[:, pieces[p]]
        load_win.append(start(win_hbm.at[:, pieces[p]], part, win_sem.at[p]))
        fetch_acts(0, p)
    load_wout = start(wout_hbm, wout, local_sem.at[1])
    fetch_grads(0)
    load_lens = start(lens_hbm, lens, local_sem.at[3])
    load_q = start(q_hbm, qs.at[lane], local_sem.at[0])
    fetch(1)

    barrier = pltpu.get_barrier_semaphore()
    peers = [peer(t) for t in range(1, n_groups)]
    for other in peers + [buddy, across]:
        pl.semaphore_signal(barrier, inc=1, device_id={"dp": other}, device_id_type=MESH)

    row_copies = []
    for c in range(count):
        span = spans[c]
        total = jnp.zeros((rank, sizes[c]), jnp.float32)
        for p in range(PIECES):
            if c == 0:
                load_win[p].wait()
            load_acts[c, p].wait()
            if p == 0:
                fetch(c + 2)
            total = total + lax.dot_general(
                win[:, pieces[p]], acts[span, pieces[p]], NT, preferred_element_type=jnp.float32
            )
        if c == 0:
            load_wout.wait()
        load_grads[c].wait()
        other = lax.dot_general(wout[...], grads[span], NT, preferred_element_type=jnp.float32)
        both = jnp.concatenate([other, total], axis=0)
        rows[c][half, slot] = both.T.astype(jnp.bfloat16)
        if c == 0:
            load_lens.wait()
            for k in range(count):
                shape = masks[k].shape[1:]
                row_id = lax.broadcasted_iota(jnp.int32, shape, 0) - slot * ex
                lane_id = lax.broadcasted_iota(jnp.int32, shape, 1) - slot * sizes[k]
                inside = (lane_id >= 0) & (lane_id < sizes[k])
                token = lane_id + starts[k]
                first = jnp.int32(0)
                mask = jnp.zeros(shape, jnp.float32)
                for e in range(ex):
                    end = first + lens[0, e]
                    hit = inside & (row_id == e) & (token >= first) & (token < end)
                    mask = jnp.where(hit, 1.0, mask)
                    first = end
                masks[k][group] = mask
            r_id = lax.broadcasted_iota(jnp.int32, (16 * pairs, width), 0)
            c_id = lax.broadcasted_iota(jnp.int32, (16 * pairs, width), 1)
            odd = (r_id >= 8 * pairs).astype(jnp.int32)
            source = 2 * ((r_id - odd * 8 * pairs) // 8) + odd
            expand[...] = jnp.where(source == c_id, 1.0, 0.0).astype(jnp.bfloat16)
            acc[...] = jnp.zeros_like(acc)
            pl.semaphore_wait(barrier, len(peers) + 2)

            load_q.wait()
            q_copies = []
            for i, other in enumerate((across, buddy)):
                copy = pltpu.make_async_remote_copy(
                    src_ref=qs.at[lane],
                    dst_ref=qs.at[lane],
                    send_sem=q_send.at[i],
                    recv_sem=q_recv.at[i],
                    device_id={"dp": other},
                    device_id_type=MESH,
                )
                copy.start()
                q_copies.append(copy)
            mask_copies = []
            for k, t in [(k, t) for k in range(count) for t in range(1, n_groups)]:
                copy = pltpu.make_async_remote_copy(
                    src_ref=masks[k].at[group],
                    dst_ref=masks[k].at[group],
                    send_sem=mask_send.at[t - 1, k],
                    recv_sem=mask_recv.at[t - 1, k],
                    device_id={"dp": peer(t)},
                    device_id_type=MESH,
                )
                copy.start()
                mask_copies.append(copy)
        copies = []
        for t in range(1, n_groups):
            copy = pltpu.make_async_remote_copy(
                src_ref=rows[c].at[half, slot],
                dst_ref=rows[c].at[half, slot],
                send_sem=row_send.at[t - 1, c],
                recv_sem=row_recv.at[t - 1, c],
                device_id={"dp": peer(t)},
                device_id_type=MESH,
            )
            copy.start()
            copies.append(copy)
        row_copies.append(copies)

    def gather(c):
        for copy in row_copies[c]:
            copy.wait_recv()
        for h in range(n_half):
            block = rows[c][h].reshape(per_half * sizes[c], width)
            mask = masks[c][h * per_half]
            for s in range(1, per_half):
                mask = mask + masks[c][h * per_half + s]
            wide = lax.dot_general(expand[...], block, NT, preferred_element_type=jnp.float32)
            wide = wide.reshape(2 * pairs, 8, mask.shape[1]) * mask[None]
            wide = wide.reshape(16 * pairs, mask.shape[1]).astype(jnp.bfloat16)
            acc[h] += lax.dot_general(wide, block, NN, preferred_element_type=jnp.float32)

    for copy in mask_copies:
        copy.wait_recv()
    for c in range(count - 2):
        gather(c)
    q_copies[0].wait_recv()
    relay = pltpu.make_async_remote_copy(
        src_ref=qs.at[across_lane],
        dst_ref=qs.at[across_lane],
        send_sem=q_send.at[2],
        recv_sem=q_recv.at[2],
        device_id={"dp": buddy},
        device_id_type=MESH,
    )
    relay.start()
    for c in range(count - 2, count):
        gather(c)

    lower = lax.broadcasted_iota(jnp.int32, (8, width), 1) < rank
    columns = []
    for k in range(pairs):
        parts = []
        for h in range(n_half):
            even = pltpu.roll(acc[h, 8 * k : 8 * k + 8], rank, 1)
            odd_rows = acc[h, 8 * pairs + 8 * k : 8 * pairs + 8 * k + 8]
            parts.append(jnp.where(lower, even, odd_rows))
        columns.append(jnp.concatenate(parts, axis=0).astype(jnp.bfloat16))
    example_grads = jnp.concatenate(columns, axis=1)
    q_copies[1].wait_recv()
    relay.wait_recv()
    queries = qs[...].reshape(qs.shape[0] * qs.shape[1], qs.shape[2])
    scores = lax.dot_general(example_grads, queries, NT, preferred_element_type=jnp.float32)
    for s in range(n_groups):
        stage[s] = scores[s * ex : (s + 1) * ex].astype(jnp.bfloat16)
    res_copies = []
    for t in range(1, n_groups):
        copy = pltpu.make_async_remote_copy(
            src_ref=stage.at[lax.rem(group + t, n_groups)],
            dst_ref=result.at[group],
            send_sem=res_send.at[t - 1],
            recv_sem=res_recv.at[t - 1],
            device_id={"dp": peer(t)},
            device_id_type=MESH,
        )
        copy.start()
        res_copies.append(copy)
    result[group] = stage[group]
    for copy in res_copies:
        copy.wait_recv()
    cols = qs.shape[0] * qs.shape[1]
    for s in range(n_groups):
        out_vmem[:, s * cols : (s + 1) * cols] = result[s]
    store = pltpu.make_async_copy(out_vmem, out_hbm, local_sem.at[4])
    store.start()
    for copy in q_copies + [relay] + mask_copies + res_copies:
        copy.wait_send()
    for copies in row_copies:
        for copy in copies:
            copy.wait_send()
    store.wait()


def local(n, activations, out_grads, lengths, proj_in, proj_out, queries):
    tokens, ff = activations.shape
    d = out_grads.shape[1]
    rank = proj_in.shape[1]
    ex = lengths.shape[1]
    nq, params = queries.shape
    n_groups = n // GROUP
    per_half = 8 // ex
    n_half = n_groups // per_half
    sizes = [tokens * part // sum(CHUNKS) for part in CHUNKS]
    count = len(sizes)
    width = 2 * rank
    bf16, f32 = jnp.bfloat16, jnp.float32
    dma = pltpu.SemaphoreType.DMA
    others = n_groups - 1
    hbm = pl.BlockSpec(memory_space=pltpu.MemorySpace.HBM)
    return pl.pallas_call(
        functools.partial(kernel, n),
        out_shape=jax.ShapeDtypeStruct((ex, nq * n), bf16),
        in_specs=[hbm] * 6,
        out_specs=pl.BlockSpec(memory_space=pl.ANY),
        scratch_shapes=[
            pltpu.SMEM((1, ex), jnp.int32),
            pltpu.VMEM((tokens, ff), bf16),
            pltpu.VMEM((tokens, d), bf16),
            pltpu.VMEM((rank, ff), bf16),
            pltpu.VMEM((rank, d), bf16),
            pltpu.VMEM((GROUP, nq, params), bf16),
            pltpu.VMEM((8 * rank, width), bf16),
            pltpu.VMEM((n_half, 8 * rank, width), f32),
            pltpu.VMEM((n_groups, ex, GROUP * nq), bf16),
            pltpu.VMEM((n_groups, ex, GROUP * nq), bf16),
            pltpu.VMEM((ex, nq * n), bf16),
            dma((5,)),
            dma((count, PIECES)),
            dma((count,)),
            dma((PIECES,)),
            dma((3,)),
            dma((3,)),
            dma((others, count)),
            dma((others, count)),
            dma((others, count)),
            dma((others, count)),
            dma((others,)),
            dma((others,)),
        ]
        + [pltpu.VMEM((n_half, per_half, size, width), bf16) for size in sizes]
        + [pltpu.VMEM((n_groups, 8, per_half * size), f32) for size in sizes],
        compiler_params=pltpu.CompilerParams(
            collective_id=0, has_side_effects=True, vmem_limit_bytes=67000000
        ),
    )(lengths, activations, out_grads, proj_in.T, proj_out.T, queries)


def solution(mesh):
    in_specs = (
        P(("parts", "dp"), None),
        P(("parts", "dp"), None),
        P(("parts", "dp"), None),
        P(),
        P(),
        P(("parts", "dp"), None),
    )
    out_specs = P(("parts", "dp"), None)
    body = functools.partial(local, mesh.shape["dp"])
    return jax.shard_map(body, mesh=mesh, in_specs=in_specs, out_specs=out_specs, check_vma=False)
```

time: 24.5 us -> 22.9 us (0.935)
  Pallas kernels: 23 us -> 21.5 us
    pallas_call x1, Pallas kernels: 23 us -> 21.5 us  [local(): pl.pallas_call(functools.partial(kernel, n), out_shape=jax.ShapeDtypeStru...]
where the time goes in v2:
time: 22.9 us; the launch traced here: 22.8 us
  Pallas kernels  21.5 us (94%)
  local copies, waits for them, and re-layouts  1.28 us (6%)
    pallas_call x1, Pallas kernels, local(): pl.pallas_call(functools.partial(kernel, n), out_shape=jax.ShapeDtypeStru...  21.5 us
    unnamed x1, local copies, waits for them, and re-layouts  1.28 us

profile of v2, /device:TPU:0, one launch (start us, length us, event | category | flops | bytes accessed | tf_op | source)
XLA Modules:
  0.0 22.8 jit_solution(8283430194508286222)
XLA Ops:
  0.0 21.5 %shard_map.64 = bf16[4,512]{1,0:T(4,128)(2,1)} custom-call(s32[1,4]{1,0:T(1,128)} %lens_hbm.1, bf16[256,14336]{1,0:T(8,128)(2,1)} %acts_hbm.1, bf16[256,4096]{1,0:T(8,128)(2,1)} %grads_hbm.1, bf16[64,14336]{1,0:T(8,128)(2,1)} %bitcast.2, bf16[64,4096]{1,0:T(8,128)(2,1)} %bitcast.3, bf16[32,4096]{1,0:T(8,128)(2,1)} %q_hbm.1), custom_call_target="tpu_custom_call" | custom-call | tf_op jit(solution)/shard_map/pallas_call | solution.py:285
  21.5 1.3 %copy.8 = bf16[4,512]{1,0:T(4,128)(2,1)} copy(bf16[4,512]{1,0:T(4,128)(2,1)} %shard_map.64) | data formatting | bytes 8192

commit v3 on v2

--- a/solution.py
+++ b/solution.py
@@ -10,7 +10,7 @@
 MESH = pl.DeviceIdType.MESH
 NT = (((1,), (1,)), ((), ()))
 NN = (((1,), (0,)), ((), ()))
-CHUNKS = (4, 8, 4)
+CHUNKS = (4, 4, 4, 4)
 PIECES = 4
 GROUP = 4
 
@@ -64,7 +64,13 @@
     ff = acts.shape[1]
     piece = ff // PIECES
 
+    backward = (group < n_groups - group).astype(jnp.int32)
+
+    def turn(t):
+        return t + backward * (n_groups - 2 * t)
+
     def peer(t):
+        t = turn(t)
         return lax.rem(group + t, n_groups) * GROUP + lane
 
     buddy = me + 1 - 2 * lax.rem(me, 2)
@@ -171,8 +177,8 @@
                 copy = pltpu.make_async_remote_copy(
                     src_ref=masks[k].at[group],
                     dst_ref=masks[k].at[group],
-                    send_sem=mask_send.at[t - 1, k],
-                    recv_sem=mask_recv.at[t - 1, k],
+                    send_sem=mask_send.at[turn(t) - 1, k],
+                    recv_sem=mask_recv.at[turn(t) - 1, k],
                     device_id={"dp": peer(t)},
                     device_id_type=MESH,
                 )
@@ -183,8 +189,8 @@
             copy = pltpu.make_async_remote_copy(
                 src_ref=rows[c].at[half, slot],
                 dst_ref=rows[c].at[half, slot],
-                send_sem=row_send.at[t - 1, c],
-                recv_sem=row_recv.at[t - 1, c],
+                send_sem=row_send.at[turn(t) - 1, c],
+                recv_sem=row_recv.at[turn(t) - 1, c],
                 device_id={"dp": peer(t)},
                 device_id_type=MESH,
             )
@@ -241,10 +247,10 @@
     res_copies = []
     for t in range(1, n_groups):
         copy = pltpu.make_async_remote_copy(
-            src_ref=stage.at[lax.rem(group + t, n_groups)],
+            src_ref=stage.at[lax.rem(group + turn(t), n_groups)],
             dst_ref=result.at[group],
-            send_sem=res_send.at[t - 1],
-            recv_sem=res_recv.at[t - 1],
+            send_sem=res_send.at[turn(t) - 1],
+            recv_sem=res_recv.at[turn(t) - 1],
             device_id={"dp": peer(t)},
             device_id_type=MESH,
         )
@@ -315,9 +321,9 @@
         + [pltpu.VMEM((n_half, per_half, size, width), bf16) for size in sizes]
         + [pltpu.VMEM((n_groups, 8, per_half * size), f32) for size in sizes],
         compiler_params=pltpu.CompilerParams(
-            collective_id=0, has_side_effects=True, vmem_limit_bytes=67000000
+            collective_id=0, has_side_effects=True, vmem_limit_bytes=56500000
         ),
-    )(lengths, activations, out_grads, proj_in.T, proj_out.T, queries)
+    )(pltpu.with_memory_space_constraint(lengths, pltpu.HBM), activations, out_grads, proj_in.T, proj_out.T, queries)
 
 
 def solution(mesh):

time: 22.9 us -> 21 us (0.917)
  Pallas kernels: 21.5 us -> 20.3 us
  local copies, waits for them, and re-layouts: 1.28 us -> 0.6 us
    pallas_call x1, Pallas kernels: 21.5 us -> 20.3 us  [local(): pl.pallas_call(functools.partial(kernel, n), out_shape=jax.ShapeDtypeStru...]
    unnamed x1, local copies, waits for them, and re-layouts: 1.28 us -> 0.6 us
where the time goes in v3:
time: 21 us; the launch traced here: 20.9 us
  Pallas kernels  20.3 us (97%)
  local copies, waits for them, and re-layouts  0.6 us (3%)
    pallas_call x1, Pallas kernels, local(): pl.pallas_call(functools.partial(kernel, n), out_shape=jax.ShapeDtypeStru...  20.3 us
    unnamed x1, local copies, waits for them, and re-layouts  0.6 us

profile of v3, /device:TPU:0, one launch (start us, length us, event | category | flops | bytes accessed | tf_op | source)
XLA Modules:
  0.0 20.9 jit_solution(3430568902191630443)
XLA Ops:
  0.0 20.3 %shard_map.64 = bf16[4,512]{1,0:T(4,128)(2,1)S(1)} custom-call(s32[1,4]{1,0:T(1,128)} %lens_hbm.1, bf16[256,14336]{1,0:T(8,128)(2,1)} %acts_hbm.1, bf16[256,4096]{1,0:T(8,128)(2,1)} %grads_hbm.1, bf16[64,14336]{1,0:T(8,128)(2,1)} %bitcast.2, bf16[64,4096]{1,0:T(8,128)(2,1)} %bitcast.3, bf16[32,4096]{1,0:T(8,128)(2,1)} %q_hbm.1), custom_call_target="tpu_custom_call" | custom-call | tf_op jit(solution)/shard_map/pallas_call | solution.py:291
  20.3 0.6 %copy.8 = bf16[4,512]{1,0:T(4,128)(2,1)} copy(bf16[4,512]{1,0:T(4,128)(2,1)S(1)} %shard_map.64) | data formatting | bytes 8192

commit v4 on v3

--- a/solution.py
+++ b/solution.py
@@ -10,7 +10,7 @@
 MESH = pl.DeviceIdType.MESH
 NT = (((1,), (1,)), ((), ()))
 NN = (((1,), (0,)), ((), ()))
-CHUNKS = (4, 4, 4, 4)
+CHUNKS = (4, 4, 5, 3)
 PIECES = 4
 GROUP = 4
 

time: 21 us -> 21.5 us (1.024)
  Pallas kernels: 20.3 us -> 20.7 us
    pallas_call x1, Pallas kernels: 20.3 us -> 20.7 us  [local(): pl.pallas_call(functools.partial(kernel, n), out_shape=jax.ShapeDtypeStru...]
where the time goes in v4:
time: 21.5 us; the launch traced here: 21.3 us
  Pallas kernels  20.7 us (96%)
  local copies, waits for them, and re-layouts  0.6 us (3%)
    pallas_call x1, Pallas kernels, local(): pl.pallas_call(functools.partial(kernel, n), out_shape=jax.ShapeDtypeStru...  20.7 us
    unnamed x1, local copies, waits for them, and re-layouts  0.6 us

profile of v4, /device:TPU:0, one launch (start us, length us, event | category | flops | bytes accessed | tf_op | source)
XLA Modules:
  0.0 21.3 jit_solution(2633589325882225)
XLA Ops:
  0.0 20.7 %shard_map.64 = bf16[4,512]{1,0:T(4,128)(2,1)S(1)} custom-call(s32[1,4]{1,0:T(1,128)} %lens_hbm.1, bf16[256,14336]{1,0:T(8,128)(2,1)} %acts_hbm.1, bf16[256,4096]{1,0:T(8,128)(2,1)} %grads_hbm.1, bf16[64,14336]{1,0:T(8,128)(2,1)} %bitcast.2, bf16[64,4096]{1,0:T(8,128)(2,1)} %bitcast.3, bf16[32,4096]{1,0:T(8,128)(2,1)} %q_hbm.1), custom_call_target="tpu_custom_call" | custom-call | tf_op jit(solution)/shard_map/pallas_call | solution.py:291
  20.7 0.6 %copy.8 = bf16[4,512]{1,0:T(4,128)(2,1)} copy(bf16[4,512]{1,0:T(4,128)(2,1)S(1)} %shard_map.64) | data formatting | bytes 8192
